TPU v7x, 256 devices: a whole 4x4x8 slice. The times are simulated.
256 devices in a mesh: series: 8 (over x_hi, y), tm: 32 (over z, x_lo, core).
Axes of the slice: x: 4 (x_hi: 2, x_lo: 2; x = x_hi * 2 + x_lo), y: 4, z: 8, core: 2. Of those that a mesh axis runs over, the one named last changes fastest.
Arguments:
- observed: bfloat16 [16384, 32768], P('series', 'tm'), may hold values from -6 to 6
- mask: bfloat16 [16384, 32768], P('series', 'tm'), may hold values from 0 to 1, as said below
- loadings: float32 [16384, 128], P('series'), may hold values from -0.5 to 0.5
- factors: float32 [32768, 128], P('tm'), may hold values from -6 to 6
- lag_weights: float32 [2, 128], replicated, may hold values from 0.2 to 0.7
Outputs:
- new_loadings: float32 [16384, 128], P('series')
- new_factors: float32 [32768, 128], P('tm')
Inputs may be any that keep to these rules, and one draw needn't show every extreme that they name: `mask`: each entry is 0 or 1.
All inputs are finite; a program needn't handle non-finite values.
Results may differ from a plain program's by a relative error of at most 0.0041.
Values sent between devices are 32-bit elements; how exact they have to be, the bound alone decides.
A program may use at most 128 MiB of HBM per device.

v0:
```python
import jax
import jax.numpy as jnp
from jax import lax
from jax.sharding import PartitionSpec as P

LAG = 1440
OUTER = 2
TIME_STEPS = 2


smooth = 4.0
shrink = 0.1
margin = 32.0


def shifted(value, axis, steps):
    count = lax.axis_size(axis)
    initial, last = (max(0, -steps), min(count, count - steps))
    return lax.ppermute(value, axis, [(source, source + steps) for source in range(initial, last)])


def split_up(x, dim, devices):
    before, after = (x.shape[:dim], x.shape[dim + 1 :])
    return jnp.moveaxis(x.reshape(*before, devices, -1, *after), dim, 0)


def sent_and_summed(x, axis, dim):
    pieces = split_up(x, dim, lax.axis_size(axis))
    arrived = lax.all_to_all(pieces, axis, split_axis=0, concat_axis=0, tiled=True)
    return arrived.sum(axis=0)


def in_order(pieces, dim):
    dims = list(pieces.shape[1:])
    dims[dim] *= pieces.shape[0]
    return jnp.moveaxis(pieces, 0, dim).reshape(dims)


def copy_for_each(x, axis):
    devices = lax.axis_size(axis)
    return lax.all_to_all(jnp.broadcast_to(x[None], (devices, *x.shape)), axis, 0, 0, tiled=True)


def gathered_copies(x, axis, dim):
    return in_order(copy_for_each(x, axis), dim)


def tile_residual(observed, mask, fb, xb):
    prod = lax.dot_general(fb, xb, (((1,), (1,)), ((), ())), preferred_element_type=jnp.float32)
    return (mask.astype(jnp.float32) * (prod - observed.astype(jnp.float32))).astype(jnp.bfloat16)


def smoothing(times, lag_weights):
    minutes = times.shape[0]
    whole = LAG // minutes
    rest = LAG % minutes
    before_one = jnp.concatenate(
        [shifted(times[minutes - 1 :], "tm", 1), times[: minutes - 1]], axis=0
    )
    before_far = jnp.concatenate(
        [
            shifted(times[minutes - rest :], "tm", whole + 1),
            shifted(times[: minutes - rest], "tm", whole),
        ],
        axis=0,
    )
    resid = times - lag_weights[0] * before_one - lag_weights[1] * before_far
    after_one = jnp.concatenate([resid[1:], shifted(resid[:1], "tm", -1)], axis=0)
    after_far = jnp.concatenate(
        [shifted(resid[rest:], "tm", -whole), shifted(resid[:rest], "tm", -(whole + 1))], axis=0
    )
    return smooth * (resid - lag_weights[0] * after_one - lag_weights[1] * after_far)


def body(observed, mask, loadings, factors, lag_weights):
    total_series = loadings.shape[0] * lax.axis_size("series")
    total_minutes = factors.shape[0] * lax.axis_size("tm")
    rank_width = loadings.shape[1]
    step_time = 1.0 / (total_series / rank_width + margin)
    step_load = 1.0 / total_minutes
    loads = loadings
    times = factors
    for outer in range(OUTER):
        fb = loads.astype(jnp.bfloat16)
        for inner in range(TIME_STEPS):
            xb = times.astype(jnp.bfloat16)
            rb = tile_residual(observed, mask, fb, xb)
            partial_grad = lax.dot_general(
                rb, fb, (((0,), (0,)), ((), ())), preferred_element_type=jnp.float32
            )
            smooth_grad = smoothing(times, lag_weights)
            share = sent_and_summed(partial_grad, "series", 0)
            rows = share.shape[0]
            start = lax.axis_index("series") * rows
            own = lax.dynamic_slice_in_dim(times, start, rows, 0)
            own_smooth = lax.dynamic_slice_in_dim(smooth_grad, start, rows, 0)
            updated = own - step_time * (share + own_smooth)
            times = gathered_copies(updated, "series", 0)
        xb = times.astype(jnp.bfloat16)
        rb = tile_residual(observed, mask, fb, xb)
        partial_load = jnp.dot(rb, xb, preferred_element_type=jnp.float32)
        share_f = sent_and_summed(partial_load, "tm", 0)
        rows_f = share_f.shape[0]
        start_f = lax.axis_index("tm") * rows_f
        own_f = lax.dynamic_slice_in_dim(loads, start_f, rows_f, 0)
        updated_f = own_f - step_load * (share_f + shrink * own_f)
        loads = gathered_copies(updated_f, "tm", 0)
    return (loads, times)


def solution(mesh):
    in_specs = (P("series", "tm"), P("series", "tm"), P("series", None), P("tm", None), P())
    out_specs = (P("series", None), P("tm", None))
    return jax.shard_map(body, mesh=mesh, in_specs=in_specs, out_specs=out_specs, check_vma=False)
```

profile of v0, /device:TPU:1, one launch (start us, length us, event | category | flops | bytes accessed | tf_op | source)
XLA Modules:
  0.0 407.9 jit_solution(16747363186595285664)
XLA Ops:
  1.6 4.5 %collective-permute-start.2 = (f32[608,128]{1,0:T(8,128)S(1)}, f32[608,128]{1,0:T(8,128)S(1)}, u32[]{:S(2)}, u32[]{:S(2)}) collective-permute-start(f32[608,128]{1,0:T(8,128)S(1)} %slice.121), channel_id=1, source_target_pairs={{0,1},{1,2},{2,3},{3,4},{4,5},{5,6},{6,7},{7,8},{8,9},{9,10},{10,1... | collective-permute-start | bytes 933896 | tf_op jit(solution)/shard_map/ppermute | solution.py:19
  6.1 6.6 %copy.12 = bf16[2048,1024]{0,1:T(8,128)(2,1)} copy(bf16[2048,1024]{1,0:T(8,128)(2,1)} %param.6) | data formatting | bytes 8388608 | tf_op args[1]
  12.7 6.6 %copy.13 = bf16[2048,1024]{0,1:T(8,128)(2,1)} copy(bf16[2048,1024]{1,0:T(8,128)(2,1)} %param.5) | data formatting | bytes 8388608 | tf_op args[0]
  19.4 6.7 %fusion.7 = f32[1024,128]{1,0:T(8,128)} fusion(bf16[2048,1024]{0,1:T(8,128)(2,1)} %copy.12, bf16[2048,1024]{0,1:T(8,128)(2,1)} %copy.13, f32[1024,128]{1,0:T(8,128)S(1)} %copy-done.2, f32[2048,128]{1,0:T(8,128)S(1)} %copy-done.1), kind=kOutput, calls=%fused_computation.19 | convolution fusion | flops 1084882944 | bytes 10485760 | tf_op jit(solution)/shard_map/dot_general | solution.py:88
  26.1 6.4 %all-to-all-start = ((f32[8,128,128]{2,1,0:T(8,128)}), f32[8,128,128]{2,1,0:T(8,128)S(1)}, u32[]{:S(2)}, u32[]{:S(2)}) async-start(f32[8,128,128]{2,1,0:T(8,128)} %bitcast), calls=%async_computation | async-start | bytes 1048576 | tf_op jit(solution)/shard_map/all_to_all | solution.py:29
  34.4 4.1 %collective-permute-start.1 = (f32[416,128]{1,0:T(8,128)S(1)}, f32[416,128]{1,0:T(8,128)S(1)}, u32[]{:S(2)}, u32[]{:S(2)}) collective-permute-start(f32[416,128]{1,0:T(8,128)S(1)} %slice.120), channel_id=1, source_target_pairs={{0,2},{1,3},{2,4},{3,5},{4,6},{5,7},{6,8},{7,9},{8,10},{9,11},{10,... | collective-permute-start | bytes 638984 | tf_op jit(solution)/shard_map/ppermute | solution.py:19
  38.6 4.9 %collective-permute-done.1 = f32[416,128]{1,0:T(8,128)S(1)} collective-permute-done((f32[416,128]{1,0:T(8,128)S(1)}, f32[416,128]{1,0:T(8,128)S(1)}, u32[]{:S(2)}, u32[]{:S(2)}) %collective-permute-start.1) | collective-permute-done | bytes 213024 | tf_op jit(solution)/shard_map/ppermute | solution.py:19
  44.4 2.4 collective-permute-start.4
  50.8 7.8 %collective-permute-done.3 = f32[1,128]{1,0:T(1,128)S(1)} collective-permute-done((f32[1,128]{1,0:T(1,128)S(1)}, f32[1,128]{1,0:T(1,128)S(1)}, u32[]{:S(2)}, u32[]{:S(2)}) %collective-permute-start.3) | collective-permute-done | bytes 544 | tf_op jit(solution)/shard_map/ppermute | solution.py:19
  58.7 17.6 %all_to_all.60 = f32[8,128,128]{2,1,0:T(8,128)S(1)} all-to-all(f32[8,128,128]{2,1,0:T(8,128)S(1)} %broadcast_in_dim.12), channel_id=1, replica_groups=mesh['series'=8,'tm'=32] {'series'}, dimensions={0} | all-to-all | bytes 1048576 | tf_op jit(solution)/shard_map/all_to_all | solution.py:41
  76.3 5.6 %collective-permute-start.6 = (f32[1,128]{1,0:T(1,128)S(1)}, f32[1,128]{1,0:T(1,128)S(1)}, u32[]{:S(2)}, u32[]{:S(2)}) collective-permute-start(f32[1,128]{1,0:T(1,128)S(1)} %slice.154), channel_id=1, source_target_pairs={{0,1},{1,2},{2,3},{3,4},{4,5},{5,6},{6,7},{7,8},{8,9},{9,10},{10,1... | collective-permute-start | bytes 1544 | tf_op jit(solution)/shard_map/ppermute | solution.py:19
  83.8 3.4 collective-permute-start.7
  87.3 6.7 %fusion.6 = f32[1024,128]{1,0:T(8,128)} fusion(bf16[2048,1024]{0,1:T(8,128)(2,1)} %copy.12, bf16[2048,1024]{0,1:T(8,128)(2,1)} %copy.13, f32[1024,128]{1,0:T(8,128)S(1)} %bitcast.80, f32[2048,128]{1,0:T(8,128)S(1)} %copy-done.1), kind=kOutput, calls=%fused_computation.18 | convolution fusion | flops 1084882944 | bytes 10485760 | tf_op jit(solution)/shard_map/dot_general | solution.py:88
  94.0 3.5 all-to-all-start.2
  98.4 2.7 collective-permute-start.10
  103.1 1.9 collective-permute-start.9
  107.0 6.8 %collective-permute-done.9 = f32[1,128]{1,0:T(1,128)S(1)} collective-permute-done((f32[1,128]{1,0:T(1,128)S(1)}, f32[1,128]{1,0:T(1,128)S(1)}, u32[]{:S(2)}, u32[]{:S(2)}) %collective-permute-start.9) | collective-permute-done | bytes 544 | tf_op jit(solution)/shard_map/ppermute | solution.py:19
  114.0 17.9 %all_to_all.61 = f32[8,128,128]{2,1,0:T(8,128)S(1)} all-to-all(f32[8,128,128]{2,1,0:T(8,128)S(1)} %broadcast_in_dim.13), channel_id=1, replica_groups=mesh['series'=8,'tm'=32] {'series'}, dimensions={0} | all-to-all | bytes 1048576 | tf_op jit(solution)/shard_map/all_to_all | solution.py:41
  131.8 6.9 %fusion.2 = bf16[2048,1024]{0,1:T(8,128)(2,1)} fusion(bf16[2048,1024]{0,1:T(8,128)(2,1)} %copy.12, bf16[2048,1024]{0,1:T(8,128)(2,1)} %copy.13, f32[1024,128]{1,0:T(8,128)S(1)} %bitcast.57, f32[2048,128]{1,0:T(8,128)S(1)} %copy-done.1), kind=kOutput, calls=%fused_computation.14 | convolution fusion | flops 547749888 | bytes 14155776 | tf_op jit(solution)/shard_map/dot_general | solution.py:49
  138.8 6.4 %copy.14 = bf16[2048,1024]{1,0:T(8,128)(2,1)} copy(bf16[2048,1024]{0,1:T(8,128)(2,1)} %fusion.2) | data formatting | bytes 8388608 | tf_op jit(solution)/shard_map/convert_element_type | solution.py:50
  145.2 4.4 %fusion.66 = f32[32,64,128]{2,1,0:T(8,128)} fusion(bf16[32,64,1024]{2,1,0:T(8,128)(2,1)} %bitcast.70, bf16[1024,128,1]{1,0,2:T(8,128)(2,1)S(1)} %bitcast.87), kind=kOutput, calls=%fused_computation.102 | convolution fusion | flops 536870912 | bytes 5505024 | tf_op jit(solution)/shard_map/dot_general | solution.py:101
  149.6 10.1 %all-to-all-start.4 = ((f32[32,64,128]{2,1,0:T(8,128)}), f32[32,64,128]{2,1,0:T(8,128)S(1)}, u32[]{:S(2)}, u32[]{:S(2)}) async-start(f32[32,64,128]{2,1,0:T(8,128)} %fusion.66), calls=%async_computation.4 | async-start | bytes 2097152 | tf_op jit(solution)/shard_map/all_to_all | solution.py:29
  159.7 28.1 %all-to-all-done.4 = f32[32,64,128]{2,1,0:T(8,128)S(1)} async-done(((f32[32,64,128]{2,1,0:T(8,128)}), f32[32,64,128]{2,1,0:T(8,128)S(1)}, u32[]{:S(2)}, u32[]{:S(2)}) %all-to-all-start.4) | async-done | bytes 1048608 | tf_op jit(solution)/shard_map/all_to_all | solution.py:29
  188.9 4.5 %all-to-all-start.5 = ((f32[32,64,128]{2,1,0:T(8,128)}), f32[32,64,128]{2,1,0:T(8,128)S(1)}, u32[]{:S(2)}, u32[]{:S(2)}) async-start(f32[32,64,128]{2,1,0:T(8,128)} %broadcast_in_dim.14), calls=%async_computation.5 | async-start | bytes 2097152 | tf_op jit(solution)/shard_map/all_to_all | solution.py:41
  193.5 3.8 collective-permute-start.12
  199.2 3.0 collective-permute-start.13
  202.2 19.2 %all-to-all-done.5 = f32[32,64,128]{2,1,0:T(8,128)S(1)} async-done(((f32[32,64,128]{2,1,0:T(8,128)}), f32[32,64,128]{2,1,0:T(8,128)S(1)}, u32[]{:S(2)}, u32[]{:S(2)}) %all-to-all-start.5) | async-done | bytes 1048608 | tf_op jit(solution)/shard_map/all_to_all | solution.py:41
  221.6 4.9 %fusion.3 = bf16[2048,1024]{0,1:T(8,128)(2,1)S(1)} fusion(bf16[2048,1024]{0,1:T(8,128)(2,1)} %copy.12, bf16[2048,1024]{0,1:T(8,128)(2,1)} %copy.13, bf16[2048,128]{1,0:T(8,128)(2,1)S(1)} %bitcast.63, bf16[1024,128]{1,0:T(8,128)(2,1)S(1)} %bitcast.88), kind=kOutput, calls=%fused_computation.15 | convolution fusion | flops 547356672 | bytes 13369344 | tf_op jit(solution)/shard_map/dot_general | solution.py:49
  226.5 2.0 fusion.67
  228.5 4.1 %all-to-all-start.6 = ((f32[8,128,128]{2,1,0:T(8,128)}), f32[8,128,128]{2,1,0:T(8,128)}, u32[]{:S(2)}, u32[]{:S(2)}) async-start(f32[8,128,128]{2,1,0:T(8,128)} %fusion.67), calls=%async_computation.6 | async-start | bytes 1048576 | tf_op jit(solution)/shard_map/all_to_all | solution.py:29
  233.6 3.4 collective-permute-start.16
  242.5 7.3 %collective-permute-done.15 = f32[1,128]{1,0:T(1,128)S(1)} collective-permute-done((f32[1,128]{1,0:T(1,128)S(1)}, f32[1,128]{1,0:T(1,128)S(1)}, u32[]{:S(2)}, u32[]{:S(2)}) %collective-permute-start.15) | collective-permute-done | bytes 544 | tf_op jit(solution)/shard_map/ppermute | solution.py:19
  249.9 17.9 %all_to_all.62 = f32[8,128,128]{2,1,0:T(8,128)S(1)} all-to-all(f32[8,128,128]{2,1,0:T(8,128)S(1)} %broadcast_in_dim.15), channel_id=1, replica_groups=mesh['series'=8,'tm'=32] {'series'}, dimensions={0} | all-to-all | bytes 1048576 | tf_op jit(solution)/shard_map/all_to_all | solution.py:41
  267.9 3.7 fusion.4
  271.7 3.7 collective-permute-start.18
  277.3 3.9 collective-permute-start.19
  281.2 2.0 fusion.68
  283.3 4.1 %all-to-all-start.8 = ((f32[8,128,128]{2,1,0:T(8,128)}), f32[8,128,128]{2,1,0:T(8,128)}, u32[]{:S(2)}, u32[]{:S(2)}) async-start(f32[8,128,128]{2,1,0:T(8,128)} %fusion.68), calls=%async_computation.8 | async-start | bytes 1048576 | tf_op jit(solution)/shard_map/all_to_all | solution.py:29
  288.3 2.7 collective-permute-start.22
  295.0 2.0 all-to-all-done.8
  298.0 4.4 %collective-permute-done.21 = f32[1,128]{1,0:T(1,128)S(1)} collective-permute-done((f32[1,128]{1,0:T(1,128)S(1)}, f32[1,128]{1,0:T(1,128)S(1)}, u32[]{:S(2)}, u32[]{:S(2)}) %collective-permute-start.21) | collective-permute-done | bytes 544 | tf_op jit(solution)/shard_map/ppermute | solution.py:19
  302.6 17.4 %all_to_all.63 = f32[8,128,128]{2,1,0:T(8,128)S(1)} all-to-all(f32[8,128,128]{2,1,0:T(8,128)S(1)} %broadcast_in_dim.16), channel_id=1, replica_groups=mesh['series'=8,'tm'=32] {'series'}, dimensions={0} | all-to-all | bytes 1048576 | tf_op jit(solution)/shard_map/all_to_all | solution.py:41
  320.0 6.9 %fusion.5 = bf16[2048,1024]{0,1:T(8,128)(2,1)} fusion(bf16[2048,1024]{0,1:T(8,128)(2,1)} %copy.12, bf16[2048,1024]{0,1:T(8,128)(2,1)} %copy.13, bf16[2048,128]{1,0:T(8,128)(2,1)S(1)} %bitcast.67, bf16[1024,128]{1,0:T(8,128)(2,1)S(1)} %bitcast.89), kind=kOutput, calls=%fused_computation.17 | convolution fusion | flops 547356672 | bytes 13369344 | tf_op jit(solution)/shard_map/dot_general | solution.py:49
  326.9 6.4 %copy.16 = bf16[2048,1024]{1,0:T(8,128)(2,1)} copy(bf16[2048,1024]{0,1:T(8,128)(2,1)} %fusion.5) | data formatting | bytes 8388608 | tf_op jit(solution)/shard_map/convert_element_type | solution.py:50
  333.3 3.5 fusion.69
  336.8 34.6 %all_to_all.64 = f32[32,64,128]{2,1,0:T(8,128)} all-to-all(f32[32,64,128]{2,1,0:T(8,128)S(1)} %fusion.69), channel_id=1, replica_groups=mesh['series'=8,'tm'=32] {'tm'}, dimensions={0} | all-to-all | bytes 2097152 | tf_op jit(solution)/shard_map/all_to_all | solution.py:29
  373.8 4.3 %all-to-all-start.11 = ((f32[32,64,128]{2,1,0:T(8,128)}), f32[32,64,128]{2,1,0:T(8,128)S(1)}, u32[]{:S(2)}, u32[]{:S(2)}) async-start(f32[32,64,128]{2,1,0:T(8,128)} %broadcast_in_dim.17), calls=%async_computation.11 | async-start | bytes 2097152 | tf_op jit(solution)/shard_map/all_to_all | solution.py:41
  378.2 28.0 %all-to-all-done.11 = f32[32,64,128]{2,1,0:T(8,128)S(1)} async-done(((f32[32,64,128]{2,1,0:T(8,128)}), f32[32,64,128]{2,1,0:T(8,128)S(1)}, u32[]{:S(2)}, u32[]{:S(2)}) %all-to-all-start.11) | async-done | bytes 1048608 | tf_op jit(solution)/shard_map/all_to_all | solution.py:41
  (98 shorter events, 36.7 us)
Async XLA Ops:
  1.6 41.9 %collective-permute-start.2 = (f32[608,128]{1,0:T(8,128)S(1)}, f32[608,128]{1,0:T(8,128)S(1)}, u32[]{:S(2)}, u32[]{:S(2)}) collective-permute-start(f32[608,128]{1,0:T(8,128)S(1)} %slice.121), channel_id=1, source_target_pairs={{0,1},{1,2},{2,3},{3,4},{4,5},{5,6},{6,7},{7,8},{8,9},{9,10},{10,1... | collective-permute-start | bytes 933896 | tf_op jit(solution)/shard_map/ppermute | solution.py:19
  12.7 6.6 %copy-start.1 = (f32[2048,128]{1,0:T(8,128)S(1)}, f32[2048,128]{1,0:T(8,128)}, u32[]{:S(2)}) copy-start(f32[2048,128]{1,0:T(8,128)} %param.7) | copy-start | bytes 3145732
  12.7 6.6 %copy-start.2 = (f32[1024,128]{1,0:T(8,128)S(1)}, f32[1024,128]{1,0:T(8,128)}, u32[]{:S(2)}) copy-start(f32[1024,128]{1,0:T(8,128)} %param.8) | copy-start | bytes 1572868
  19.4 19.2 %copy-start.3 = (f32[2,128]{1,0:T(2,128)S(1)}, f32[2,128]{1,0:T(2,128)}, u32[]{:S(2)}) copy-start(f32[2,128]{1,0:T(2,128)} %param.9) | copy-start | bytes 3076
  26.1 24.6 %all-to-all-start = ((f32[8,128,128]{2,1,0:T(8,128)}), f32[8,128,128]{2,1,0:T(8,128)S(1)}, u32[]{:S(2)}, u32[]{:S(2)}) async-start(f32[8,128,128]{2,1,0:T(8,128)} %bitcast), calls=%async_computation | async-start | bytes 1048576 | tf_op jit(solution)/shard_map/all_to_all | solution.py:29
  32.5 6.1 %collective-permute-start = (f32[1,128]{1,0:T(1,128)S(1)}, f32[1,128]{1,0:T(1,128)S(1)}, u32[]{:S(2)}, u32[]{:S(2)}) collective-permute-start(f32[1,128]{1,0:T(1,128)S(1)} %slice.117), channel_id=1, source_target_pairs={{0,1},{1,2},{2,3},{3,4},{4,5},{5,6},{6,7},{7,8},{8,9},{9,10},{10,1... | collective-permute-start | bytes 1544 | tf_op jit(solution)/shard_map/ppermute | solution.py:19
  34.4 9.1 %collective-permute-start.1 = (f32[416,128]{1,0:T(8,128)S(1)}, f32[416,128]{1,0:T(8,128)S(1)}, u32[]{:S(2)}, u32[]{:S(2)}) collective-permute-start(f32[416,128]{1,0:T(8,128)S(1)} %slice.120), channel_id=1, source_target_pairs={{0,2},{1,3},{2,4},{3,5},{4,6},{5,7},{6,8},{7,9},{8,10},{9,11},{10,... | collective-permute-start | bytes 638984 | tf_op jit(solution)/shard_map/ppermute | solution.py:19
  44.4 14.2 %collective-permute-start.4 = (f32[608,128]{1,0:T(8,128)}, f32[608,128]{1,0:T(8,128)S(1)}, u32[]{:S(2)}, u32[]{:S(2)}) collective-permute-start(f32[608,128]{1,0:T(8,128)} %slice.152), channel_id=1, source_target_pairs={{1,0},{2,1},{3,2},{4,3},{5,4},{6,5},{7,6},{8,7},{9,8},{10,9},{11,1... | collective-permute-start | bytes 933896 | tf_op jit(solution)/shard_map/ppermute | solution.py:19
  47.5 11.1 %collective-permute-start.5 = (f32[416,128]{1,0:T(8,128)}, f32[416,128]{1,0:T(8,128)}, u32[]{:S(2)}, u32[]{:S(2)}) collective-permute-start(f32[416,128]{1,0:T(8,128)} %slice.153), channel_id=1, source_target_pairs={{2,0},{3,1},{4,2},{5,3},{6,4},{7,5},{8,6},{9,7},{10,8},{11,9},{12,... | collective-permute-start | bytes 638984 | tf_op jit(solution)/shard_map/ppermute | solution.py:19
  48.8 9.8 %collective-permute-start.3 = (f32[1,128]{1,0:T(1,128)S(1)}, f32[1,128]{1,0:T(1,128)S(1)}, u32[]{:S(2)}, u32[]{:S(2)}) collective-permute-start(f32[1,128]{1,0:T(1,128)S(1)} %slice.151), channel_id=1, source_target_pairs={{1,0},{2,1},{3,2},{4,3},{5,4},{6,5},{7,6},{8,7},{9,8},{10,9},{11,1... | collective-permute-start | bytes 1544 | tf_op jit(solution)/shard_map/ppermute | solution.py:19
  76.3 21.2 %collective-permute-start.6 = (f32[1,128]{1,0:T(1,128)S(1)}, f32[1,128]{1,0:T(1,128)S(1)}, u32[]{:S(2)}, u32[]{:S(2)}) collective-permute-start(f32[1,128]{1,0:T(1,128)S(1)} %slice.154), channel_id=1, source_target_pairs={{0,1},{1,2},{2,3},{3,4},{4,5},{5,6},{6,7},{7,8},{8,9},{9,10},{10,1... | collective-permute-start | bytes 1544 | tf_op jit(solution)/shard_map/ppermute | solution.py:19
  81.9 15.6 %collective-permute-start.8 = (f32[608,128]{1,0:T(8,128)S(1)}, f32[608,128]{1,0:T(8,128)S(1)}, u32[]{:S(2)}, u32[]{:S(2)}) collective-permute-start(f32[608,128]{1,0:T(8,128)S(1)} %slice.157), channel_id=1, source_target_pairs={{0,1},{1,2},{2,3},{3,4},{4,5},{5,6},{6,7},{7,8},{8,9},{9,10},{10,1... | collective-permute-start | bytes 933896 | tf_op jit(solution)/shard_map/ppermute | solution.py:19
  83.8 13.7 %collective-permute-start.7 = (f32[416,128]{1,0:T(8,128)S(1)}, f32[416,128]{1,0:T(8,128)S(1)}, u32[]{:S(2)}, u32[]{:S(2)}) collective-permute-start(f32[416,128]{1,0:T(8,128)S(1)} %slice.156), channel_id=1, source_target_pairs={{0,2},{1,3},{2,4},{3,5},{4,6},{5,7},{6,8},{7,9},{8,10},{9,11},{10,... | collective-permute-start | bytes 638984 | tf_op jit(solution)/shard_map/ppermute | solution.py:19
  94.0 12.9 %all-to-all-start.2 = ((f32[8,128,128]{2,1,0:T(8,128)}), f32[8,128,128]{2,1,0:T(8,128)S(1)}, u32[]{:S(2)}, u32[]{:S(2)}) async-start(f32[8,128,128]{2,1,0:T(8,128)} %bitcast.5), calls=%async_computation.2 | async-start | bytes 1048576 | tf_op jit(solution)/shard_map/all_to_all | solution.py:29
  98.4 15.4 %collective-permute-start.10 = (f32[608,128]{1,0:T(8,128)}, f32[608,128]{1,0:T(8,128)S(1)}, u32[]{:S(2)}, u32[]{:S(2)}) collective-permute-start(f32[608,128]{1,0:T(8,128)} %slice.160), channel_id=1, source_target_pairs={{1,0},{2,1},{3,2},{4,3},{5,4},{6,5},{7,6},{8,7},{9,8},{10,9},{11,1... | collective-permute-start | bytes 933896 | tf_op jit(solution)/shard_map/ppermute | solution.py:19
  101.8 12.0 %collective-permute-start.11 = (f32[416,128]{1,0:T(8,128)}, f32[416,128]{1,0:T(8,128)}, u32[]{:S(2)}, u32[]{:S(2)}) collective-permute-start(f32[416,128]{1,0:T(8,128)} %slice.161), channel_id=1, source_target_pairs={{2,0},{3,1},{4,2},{5,3},{6,4},{7,5},{8,6},{9,7},{10,8},{11,9},{12,... | collective-permute-start | bytes 638984 | tf_op jit(solution)/shard_map/ppermute | solution.py:19
  103.1 10.7 %collective-permute-start.9 = (f32[1,128]{1,0:T(1,128)S(1)}, f32[1,128]{1,0:T(1,128)S(1)}, u32[]{:S(2)}, u32[]{:S(2)}) collective-permute-start(f32[1,128]{1,0:T(1,128)S(1)} %slice.159), channel_id=1, source_target_pairs={{1,0},{2,1},{3,2},{4,3},{5,4},{6,5},{7,6},{8,7},{9,8},{10,9},{11,1... | collective-permute-start | bytes 1544 | tf_op jit(solution)/shard_map/ppermute | solution.py:19
  149.6 38.1 %all-to-all-start.4 = ((f32[32,64,128]{2,1,0:T(8,128)}), f32[32,64,128]{2,1,0:T(8,128)S(1)}, u32[]{:S(2)}, u32[]{:S(2)}) async-start(f32[32,64,128]{2,1,0:T(8,128)} %fusion.66), calls=%async_computation.4 | async-start | bytes 2097152 | tf_op jit(solution)/shard_map/all_to_all | solution.py:29
  188.9 32.5 %all-to-all-start.5 = ((f32[32,64,128]{2,1,0:T(8,128)}), f32[32,64,128]{2,1,0:T(8,128)S(1)}, u32[]{:S(2)}, u32[]{:S(2)}) async-start(f32[32,64,128]{2,1,0:T(8,128)} %broadcast_in_dim.14), calls=%async_computation.5 | async-start | bytes 2097152 | tf_op jit(solution)/shard_map/all_to_all | solution.py:41
  193.5 39.1 %collective-permute-start.12 = (f32[1,128]{1,0:T(1,128)S(1)}, f32[1,128]{1,0:T(1,128)S(1)}, u32[]{:S(2)}, u32[]{:S(2)}) collective-permute-start(f32[1,128]{1,0:T(1,128)S(1)} %slice.162), channel_id=1, source_target_pairs={{0,1},{1,2},{2,3},{3,4},{4,5},{5,6},{6,7},{7,8},{8,9},{9,10},{10,1... | collective-permute-start | bytes 1544 | tf_op jit(solution)/shard_map/ppermute | solution.py:19
  197.3 35.4 %collective-permute-start.14 = (f32[608,128]{1,0:T(8,128)S(1)}, f32[608,128]{1,0:T(8,128)S(1)}, u32[]{:S(2)}, u32[]{:S(2)}) collective-permute-start(f32[608,128]{1,0:T(8,128)S(1)} %slice.165), channel_id=1, source_target_pairs={{0,1},{1,2},{2,3},{3,4},{4,5},{5,6},{6,7},{7,8},{8,9},{9,10},{10,1... | collective-permute-start | bytes 933896 | tf_op jit(solution)/shard_map/ppermute | solution.py:19
  199.2 33.5 %collective-permute-start.13 = (f32[416,128]{1,0:T(8,128)S(1)}, f32[416,128]{1,0:T(8,128)S(1)}, u32[]{:S(2)}, u32[]{:S(2)}) collective-permute-start(f32[416,128]{1,0:T(8,128)S(1)} %slice.164), channel_id=1, source_target_pairs={{0,2},{1,3},{2,4},{3,5},{4,6},{5,7},{6,8},{7,9},{8,10},{9,11},{10,... | collective-permute-start | bytes 638984 | tf_op jit(solution)/shard_map/ppermute | solution.py:19
  228.5 12.9 %all-to-all-start.6 = ((f32[8,128,128]{2,1,0:T(8,128)}), f32[8,128,128]{2,1,0:T(8,128)}, u32[]{:S(2)}, u32[]{:S(2)}) async-start(f32[8,128,128]{2,1,0:T(8,128)} %fusion.67), calls=%async_computation.6 | async-start | bytes 1048576 | tf_op jit(solution)/shard_map/all_to_all | solution.py:29
  233.6 16.2 %collective-permute-start.16 = (f32[608,128]{1,0:T(8,128)}, f32[608,128]{1,0:T(8,128)S(1)}, u32[]{:S(2)}, u32[]{:S(2)}) collective-permute-start(f32[608,128]{1,0:T(8,128)} %slice.168), channel_id=1, source_target_pairs={{1,0},{2,1},{3,2},{4,3},{5,4},{6,5},{7,6},{8,7},{9,8},{10,9},{11,1... | collective-permute-start | bytes 933896 | tf_op jit(solution)/shard_map/ppermute | solution.py:19
  237.7 12.1 %collective-permute-start.17 = (f32[416,128]{1,0:T(8,128)}, f32[416,128]{1,0:T(8,128)}, u32[]{:S(2)}, u32[]{:S(2)}) collective-permute-start(f32[416,128]{1,0:T(8,128)} %slice.169), channel_id=1, source_target_pairs={{2,0},{3,1},{4,2},{5,3},{6,4},{7,5},{8,6},{9,7},{10,8},{11,9},{12,... | collective-permute-start | bytes 638984 | tf_op jit(solution)/shard_map/ppermute | solution.py:19
  239.0 10.8 %collective-permute-start.15 = (f32[1,128]{1,0:T(1,128)S(1)}, f32[1,128]{1,0:T(1,128)S(1)}, u32[]{:S(2)}, u32[]{:S(2)}) collective-permute-start(f32[1,128]{1,0:T(1,128)S(1)} %slice.167), channel_id=1, source_target_pairs={{1,0},{2,1},{3,2},{4,3},{5,4},{6,5},{7,6},{8,7},{9,8},{10,9},{11,1... | collective-permute-start | bytes 1544 | tf_op jit(solution)/shard_map/ppermute | solution.py:19
  242.5 25.4 %copy-start = (bf16[2048,1024]{0,1:T(8,128)(2,1)S(1)}, bf16[2048,1024]{0,1:T(8,128)(2,1)}, u32[]{:S(2)}) copy-start(bf16[2048,1024]{0,1:T(8,128)(2,1)} %copy.12) | copy-start | bytes 12582916
  271.7 15.8 %collective-permute-start.18 = (f32[1,128]{1,0:T(1,128)S(1)}, f32[1,128]{1,0:T(1,128)S(1)}, u32[]{:S(2)}, u32[]{:S(2)}) collective-permute-start(f32[1,128]{1,0:T(1,128)S(1)} %slice.170), channel_id=1, source_target_pairs={{0,1},{1,2},{2,3},{3,4},{4,5},{5,6},{6,7},{7,8},{8,9},{9,10},{10,1... | collective-permute-start | bytes 1544 | tf_op jit(solution)/shard_map/ppermute | solution.py:19
  275.4 12.0 %collective-permute-start.20 = (f32[608,128]{1,0:T(8,128)S(1)}, f32[608,128]{1,0:T(8,128)S(1)}, u32[]{:S(2)}, u32[]{:S(2)}) collective-permute-start(f32[608,128]{1,0:T(8,128)S(1)} %slice.173), channel_id=1, source_target_pairs={{0,1},{1,2},{2,3},{3,4},{4,5},{5,6},{6,7},{7,8},{8,9},{9,10},{10,1... | collective-permute-start | bytes 933896 | tf_op jit(solution)/shard_map/ppermute | solution.py:19
  277.3 10.1 %collective-permute-start.19 = (f32[416,128]{1,0:T(8,128)S(1)}, f32[416,128]{1,0:T(8,128)S(1)}, u32[]{:S(2)}, u32[]{:S(2)}) collective-permute-start(f32[416,128]{1,0:T(8,128)S(1)} %slice.172), channel_id=1, source_target_pairs={{0,2},{1,3},{2,4},{3,5},{4,6},{5,7},{6,8},{7,9},{8,10},{9,11},{10,... | collective-permute-start | bytes 638984 | tf_op jit(solution)/shard_map/ppermute | solution.py:19
  283.3 13.7 %all-to-all-start.8 = ((f32[8,128,128]{2,1,0:T(8,128)}), f32[8,128,128]{2,1,0:T(8,128)}, u32[]{:S(2)}, u32[]{:S(2)}) async-start(f32[8,128,128]{2,1,0:T(8,128)} %fusion.68), calls=%async_computation.8 | async-start | bytes 1048576 | tf_op jit(solution)/shard_map/all_to_all | solution.py:29
  288.3 14.1 %collective-permute-start.22 = (f32[608,128]{1,0:T(8,128)}, f32[608,128]{1,0:T(8,128)S(1)}, u32[]{:S(2)}, u32[]{:S(2)}) collective-permute-start(f32[608,128]{1,0:T(8,128)} %slice.176), channel_id=1, source_target_pairs={{1,0},{2,1},{3,2},{4,3},{5,4},{6,5},{7,6},{8,7},{9,8},{10,9},{11,1... | collective-permute-start | bytes 933896 | tf_op jit(solution)/shard_map/ppermute | solution.py:19
  291.7 10.7 %collective-permute-start.23 = (f32[416,128]{1,0:T(8,128)}, f32[416,128]{1,0:T(8,128)}, u32[]{:S(2)}, u32[]{:S(2)}) collective-permute-start(f32[416,128]{1,0:T(8,128)} %slice.177), channel_id=1, source_target_pairs={{2,0},{3,1},{4,2},{5,3},{6,4},{7,5},{8,6},{9,7},{10,8},{11,9},{12,... | collective-permute-start | bytes 638984 | tf_op jit(solution)/shard_map/ppermute | solution.py:19
  293.0 9.4 %collective-permute-start.21 = (f32[1,128]{1,0:T(1,128)S(1)}, f32[1,128]{1,0:T(1,128)S(1)}, u32[]{:S(2)}, u32[]{:S(2)}) collective-permute-start(f32[1,128]{1,0:T(1,128)S(1)} %slice.175), channel_id=1, source_target_pairs={{1,0},{2,1},{3,2},{4,3},{5,4},{6,5},{7,6},{8,7},{9,8},{10,9},{11,1... | collective-permute-start | bytes 1544 | tf_op jit(solution)/shard_map/ppermute | solution.py:19
  373.8 32.3 %all-to-all-start.11 = ((f32[32,64,128]{2,1,0:T(8,128)}), f32[32,64,128]{2,1,0:T(8,128)S(1)}, u32[]{:S(2)}, u32[]{:S(2)}) async-start(f32[32,64,128]{2,1,0:T(8,128)} %broadcast_in_dim.17), calls=%async_computation.11 | async-start | bytes 2097152 | tf_op jit(solution)/shard_map/all_to_all | solution.py:41
where the time goes:
time: 411 us; the launch traced here: 408 us
  waiting for transfers between devices  111 us (27%)
  blocking collectives  105 us (26%)
  starting transfers between devices  101 us (25%)
  matrix products  47.9 us (12%)
  local copies, waits for them, and re-layouts  37.2 us (9%)
  other arithmetic  4.57 us (1%)
    all_to_all x4, blocking collectives, copy_for_each(): lax.all_to_all(jnp.broadcast_to(x[None], (devices, *x.shape)), axis, 0, 0...  70.7 us
    ppermute x24, starting transfers between devices, shifted(): lax.ppermute(value, axis, [(source, source + steps) for source in range(i...  63.7 us
    all_to_all x2, waiting for transfers between devices, copy_for_each(): lax.all_to_all(jnp.broadcast_to(x[None], (devices, *x.shape)), axis, 0, 0...  47.2 us
    all_to_all x1, blocking collectives, sent_and_summed(): lax.all_to_all(pieces, axis, split_axis=0, concat_axis=0, tiled=True)  34.6 us
    all_to_all x5, waiting for transfers between devices, sent_and_summed(): lax.all_to_all(pieces, axis, split_axis=0, concat_axis=0, tiled=True)  32.4 us
    ppermute x24, waiting for transfers between devices, shifted(): lax.ppermute(value, axis, [(source, source + steps) for source in range(i...  31.3 us
    all_to_all x5, starting transfers between devices, sent_and_summed(): lax.all_to_all(pieces, axis, split_axis=0, concat_axis=0, tiled=True)  28.2 us
    dot_general x4, matrix products, tile_residual(): lax.dot_general(fb, xb, (((1,), (1,)), ((), ())), preferred_element_type=...  22.5 us
  transfers between devices with their start and end apart: 31, of which 11 were waited for; matrix products, arithmetic and copies ran while one was open for 11% of the time, Pallas kernels for 0%

commit v1 on v0

v1 whole, which is shorter than its diff:
```python
import functools

import jax
import jax.numpy as jnp
from jax import lax
from jax.experimental import pallas as pl
from jax.experimental.pallas import tpu as pltpu
from jax.sharding import PartitionSpec as P

LAG = 1440
OUTER = 2
TIME_STEPS = 2
STEPS = OUTER * TIME_STEPS
CHUNKS = 4

smooth = 4.0
shrink = 0.1
margin = 32.0

MESH = pl.DeviceIdType.MESH
F32 = jnp.float32
BF16 = jnp.bfloat16
NT = (((1,), (1,)), ((), ()))


def rows_of(start, size):
    return pl.ds(pl.multiple_of(start, size), size)


def kernel(
    groups, spans,
    obs_hbm, mask_hbm, loads_hbm, times_hbm, weights,
    loads_out, times_out,
    obs, mask, fs, xs, gs, hs, got_g, got_h, core_h, sum_h,
    back, ahead, edge_before, edge_after,
    fb, fbt, xb, resid, resid_f, window,
    in_sem, tile_sem, out_sem,
    g_send, g_recv, x_send, x_recv,
    halo_send, back_recv, ahead_recv, edge_recv,
    core_send, core_recv, h_send, h_recv, f_send, f_recv, pair_send, pair_recv,
):
    n_series, n_tm = groups
    series, minutes = spans
    rank = weights.shape[1]
    n_pair = n_tm // 2
    cols = minutes // CHUNKS
    own = cols // n_series
    granules = minutes // own
    far = LAG // own
    far_in = far % granules
    series_rows = series // CHUNKS
    half = series_rows // 2
    own_f = half // n_pair
    total_minutes = minutes * n_tm
    step_time = 1.0 / (series * n_series / rank + margin)
    step_load = 1.0 / total_minutes

    s = lax.axis_index("series")
    m = lax.axis_index("tm")
    core = lax.rem(m, 2)
    pair = m // 2
    partner = m + 1 - 2 * core

    def send(src, dst, send_sem, recv_sem, to_s, to_m):
        pltpu.make_async_remote_copy(
            src_ref=src, dst_ref=dst, send_sem=send_sem, recv_sem=recv_sem,
            device_id=(to_s, to_m), device_id_type=MESH,
        ).start()

    def wait_for(ref, sem):
        pltpu.make_async_copy(ref, ref, sem).wait()

    barrier = pltpu.get_barrier_semaphore()

    def greet(to_s, to_m):
        pl.semaphore_signal(barrier, inc=1, device_id=(to_s, to_m), device_id_type=MESH)

    for d in range(1, n_series):
        greet(lax.rem(s + d, n_series), m)
    for d in range(1, n_pair):
        greet(s, 2 * lax.rem(pair + d, n_pair) + core)
    greet(s, partner)
    greet(s, lax.rem(m + 1, n_tm))
    greet(s, lax.rem(m + n_tm - 1, n_tm))
    greetings = (n_series - 1) + (n_pair - 1) + 3

    times_in = pltpu.make_async_copy(times_hbm, xs.at[0], in_sem.at[0])
    loads_in = pltpu.make_async_copy(loads_hbm, fs.at[0], in_sem.at[1])
    times_in.start()
    loads_in.start()

    def tile_in(c, which):
        ref, hbm = ((obs, obs_hbm), (mask, mask_hbm))[which]
        at = rows_of(c * cols, cols)
        return pltpu.make_async_copy(hbm.at[:, at], ref.at[:, at], tile_sem.at[which, c])

    for c in range(CHUNKS):
        tile_in(c, 0).start()
        tile_in(c, 1).start()

    def halo_out(k, c):
        def place(offset, shift):
            g = c * n_series + lax.rem(s + offset, n_series)
            j = lax.rem(g + shift, granules)
            return g, j // n_series, (g + shift) // granules

        g, chunk, over = place(2 * n_series - far_in, far_in)
        send(xs.at[k, rows_of(g * own, own)], back.at[k, chunk, pl.ds(0, own)],
             halo_send.at[k, c], back_recv.at[k, chunk], s, lax.rem(m + far // granules + over, n_tm))
        g, chunk, over = place(2 * n_series - far_in + 1, far_in - 1)
        send(xs.at[k, rows_of(g * own, 8)], back.at[k, chunk, pl.ds(own, 8)],
             halo_send.at[k, c], back_recv.at[k, chunk], s, lax.rem(m + far // granules + over, n_tm))
        g, chunk, over = place(far_in, granules - far_in)
        send(xs.at[k, rows_of(g * own, own)], ahead.at[k, chunk, pl.ds(8, own)],
             halo_send.at[k, c], ahead_recv.at[k, chunk], s,
             lax.rem(m + n_tm - far // granules - 1 + over, n_tm))
        g, chunk, over = place(far_in - 1, granules - far_in + 1)
        send(xs.at[k, rows_of(g * own + own - 8, 8)], ahead.at[k, chunk, pl.ds(0, 8)],
             halo_send.at[k, c], ahead_recv.at[k, chunk], s,
             lax.rem(m + n_tm - far // granules - 1 + over, n_tm))

    def edges_out(k):
        send(xs.at[k, pl.ds(minutes - 8, 8)], edge_before.at[k],
             halo_send.at[k, CHUNKS], edge_recv.at[k, 0], s, lax.rem(m + 1, n_tm))
        send(xs.at[k, pl.ds(0, 8)], edge_after.at[k],
             halo_send.at[k, CHUNKS + 1], edge_recv.at[k, 1], s, lax.rem(m + n_tm - 1, n_tm))

    def halo_wait(k):
        for c in range(CHUNKS):
            wait_for(back.at[k, pl.ds(0, 2)], halo_send.at[k, c])
        wait_for(edge_before.at[k], halo_send.at[k, CHUNKS])
        wait_for(edge_after.at[k], halo_send.at[k, CHUNKS + 1])

    def round_times(k, c):
        at = rows_of(c * cols, cols)
        xb[at] = xs[k, at].astype(BF16)

    def round_loads(o, e):
        at = rows_of(e * series_rows, series_rows)
        block = fs[o, at]
        fb[at] = block.astype(BF16)
        fbt[:, at] = block.T.astype(BF16)

    def gradient(k, c):
        at = rows_of(c * cols, cols)
        x_block = xb[at]
        step = 256
        for i in range(series // step):
            part = pl.ds(i * step, step)
            prod = lax.dot_general(fb[part], x_block, NT, preferred_element_type=F32)
            resid[part] = (prod - obs[part, at].astype(F32)).astype(BF16) * mask[part, at]
        grad = jnp.dot(fbt[...], resid[...], preferred_element_type=F32)
        gs[k, at] = grad.T
        for d in range(1, n_series):
            to = lax.rem(s + d, n_series)
            send(gs.at[k, rows_of((c * n_series + to) * own, own)], got_g.at[k, c, n_series - 1 - d],
                 g_send.at[k, c], g_recv.at[k, c], to, m)

    def smoothing(k, c):
        wait_for(back.at[k, c], back_recv.at[k, c])
        wait_for(ahead.at[k, c], ahead_recv.at[k, c])
        j = c * n_series + s
        first = j * own
        before = xs[k, rows_of(jnp.maximum(first - 8, 0), 8)]
        after = xs[k, rows_of(jnp.minimum(first + own, minutes - 8), 8)]
        window[0:8] = jnp.where(j == 0, edge_before[k], before)
        x = xs[k, rows_of(first, own)]
        window[8:8 + own] = x
        window[8 + own:16 + own] = jnp.where(j == granules - 1, edge_after[k], after)
        t = m * minutes + first + lax.broadcasted_iota(jnp.int32, (own, rank), 0)
        w0 = weights[0:1]
        w1 = weights[1:2]
        prev = jnp.where(t >= 1, window[7:7 + own], 0.0)
        after_one = window[9:9 + own]
        back_far = jnp.where(t >= LAG, back[k, c, 0:own], 0.0)
        back_near = jnp.where(t >= LAG - 1, back[k, c, 1:1 + own], 0.0)
        here = x - w0 * prev - w1 * back_far
        one = jnp.where(t + 1 < total_minutes, after_one - w0 * x - w1 * back_near, 0.0)
        there = jnp.where(
            t + LAG < total_minutes, ahead[k, c, 8:8 + own] - w0 * ahead[k, c, 7:7 + own] - w1 * x, 0.0
        )
        return x, smooth * (here - w0 * one - w1 * there)

    def update_times(k, c):
        x, smooth_grad = smoothing(k, c)
        wait_for(got_g.at[k, c], g_recv.at[k, c])
        at = rows_of((c * n_series + s) * own, own)
        total = gs[k, at]
        for d in range(n_series - 1):
            total = total + got_g[k, c, d]
        xs[k + 1, at] = x - step_time * (total + smooth_grad)
        for d in range(1, n_series):
            send(xs.at[k + 1, at], xs.at[k + 1, at], x_send.at[k, c], x_recv.at[k, c],
                 lax.rem(s + d, n_series), m)
        wait_for(got_g.at[k, c], g_send.at[k, c])

    def times_arrived(k, c):
        wait_for(got_g.at[k, c], x_recv.at[k, c])
        wait_for(got_g.at[k, c], x_send.at[k, c])

    def each(body):
        def step(i, carry):
            body(i)
            return carry
        lax.fori_loop(0, CHUNKS, step, 0)

    def load_gradient(o, e):
        at = rows_of(e * series_rows, series_rows)
        f_block = fb[at]
        step = 256
        for i in range(minutes // step):
            part = pl.ds(i * step, step)
            prod = lax.dot_general(f_block, xb[part], NT, preferred_element_type=F32)
            resid_f[:, part] = (prod - obs[at, part].astype(F32)).astype(BF16) * mask[at, part]
        hs[o, at] = jnp.dot(resid_f[...], xb[...], preferred_element_type=F32)
        send(hs.at[o, rows_of(e * series_rows + half * (1 - core), half)], core_h.at[o, e],
             core_send.at[o, e], core_recv.at[o, e], s, partner)

    def load_share(o, e):
        wait_for(core_h.at[o, e], core_recv.at[o, e])
        sum_h[o, e] = hs[o, rows_of(e * series_rows + half * core, half)] + core_h[o, e]
        for d in range(1, n_pair):
            to = lax.rem(pair + d, n_pair)
            send(sum_h.at[o, e, rows_of(to * own_f, own_f)], got_h.at[o, e, n_pair - 1 - d],
                 h_send.at[o, e], h_recv.at[o, e], s, 2 * to + core)

    def update_loads(o, e):
        wait_for(got_h.at[o, e], h_recv.at[o, e])
        total = sum_h[o, e, rows_of(pair * own_f, own_f)]
        for d in range(n_pair - 1):
            total = total + got_h[o, e, d]
        at = rows_of(e * series_rows + half * core + pair * own_f, own_f)
        f = fs[o, at]
        fs[o + 1, at] = f - step_load * (total + shrink * f)
        for d in range(1, n_pair):
            send(fs.at[o + 1, at], fs.at[o + 1, at], f_send.at[o, e], f_recv.at[o, e],
                 s, 2 * lax.rem(pair + d, n_pair) + core)
        wait_for(core_h.at[o, e], core_send.at[o, e])
        wait_for(got_h.at[o, e], h_send.at[o, e])

    def loads_half(o, e):
        wait_for(got_h.at[o, e], f_recv.at[o, e])
        at = rows_of(e * series_rows + half * core, half)
        send(fs.at[o + 1, at], fs.at[o + 1, at], pair_send.at[o, e], pair_recv.at[o, e], s, partner)
        wait_for(got_h.at[o, e], f_send.at[o, e])

    def loads_arrived(o, e):
        wait_for(core_h.at[o, e], pair_recv.at[o, e])
        wait_for(core_h.at[o, e], pair_send.at[o, e])

    times_in.wait()
    loads_in.wait()
    for c in range(CHUNKS):
        round_times(0, c)
    pl.semaphore_wait(barrier, greetings)
    each(lambda c: halo_out(0, c))
    edges_out(0)
    each(lambda e: round_loads(0, e))

    def outer(o, carry):
        for i in range(TIME_STEPS):
            k = TIME_STEPS * o + i

            def first_half(c, k=k, i=i):
                if i == 0:
                    @pl.when(o == 0)
                    def _():
                        for which in range(2):
                            tile_in(c, which).wait()
                else:
                    times_arrived(k - 1, c)
                    halo_out(k, c)
                    round_times(k, c)
                gradient(k, c)

            each(first_half)
            if i > 0:
                edges_out(k)
            for which, ref in enumerate((edge_before, edge_after)):
                wait_for(ref.at[k], edge_recv.at[k, which])
            each(functools.partial(update_times, k))
            halo_wait(k)

        def settle(c):
            times_arrived(k, c)
            round_times(k + 1, c)

            @pl.when(o < OUTER - 1)
            def _():
                halo_out(k + 1, c)

        each(settle)

        @pl.when(o < OUTER - 1)
        def _():
            edges_out(k + 1)

        def load_first(e):
            load_gradient(o, e)

            @pl.when(e > 0)
            def _():
                load_share(o, e - 1)

        each(load_first)
        load_share(o, CHUNKS - 1)
        each(functools.partial(update_loads, o))
        each(functools.partial(loads_half, o))

        def load_last(e):
            loads_arrived(o, e)

            @pl.when(o < OUTER - 1)
            def _():
                round_loads(o + 1, e)

        each(load_last)
        return carry

    lax.fori_loop(0, OUTER, outer, 0)
    times_back = pltpu.make_async_copy(xs.at[STEPS], times_out, out_sem.at[0])
    loads_back = pltpu.make_async_copy(fs.at[OUTER], loads_out, out_sem.at[1])
    times_back.start()
    loads_back.start()
    times_back.wait()
    loads_back.wait()


def body(observed, mask, loadings, factors, lag_weights):
    n_series, n_tm = lax.axis_size("series"), lax.axis_size("tm")
    series, minutes = observed.shape
    rank = loadings.shape[1]
    cols = minutes // CHUNKS
    own = cols // n_series
    n_pair = n_tm // 2
    series_rows = series // CHUNKS
    half = series_rows // 2
    own_f = half // n_pair
    vmem = pltpu.VMEM
    dma = pltpu.SemaphoreType.DMA
    anywhere = pl.BlockSpec(memory_space=pl.ANY)
    scratch = [
        vmem((series, minutes), BF16),
        vmem((series, minutes), BF16),
        vmem((OUTER + 1, series, rank), F32),
        vmem((STEPS + 1, minutes, rank), F32),
        vmem((STEPS, minutes, rank), F32),
        vmem((OUTER, series, rank), F32),
        vmem((STEPS, CHUNKS, n_series - 1, own, rank), F32),
        vmem((OUTER, CHUNKS, n_pair - 1, own_f, rank), F32),
        vmem((OUTER, CHUNKS, half, rank), F32),
        vmem((OUTER, CHUNKS, half, rank), F32),
        vmem((STEPS, CHUNKS, own + 8, rank), F32),
        vmem((STEPS, CHUNKS, own + 8, rank), F32),
        vmem((STEPS, 8, rank), F32),
        vmem((STEPS, 8, rank), F32),
        vmem((series, rank), BF16),
        vmem((rank, series), BF16),
        vmem((minutes, rank), BF16),
        vmem((series, cols), BF16),
        vmem((series_rows, minutes), BF16),
        vmem((own + 16, rank), F32),
        dma((2,)), dma((2, CHUNKS)), dma((2,)),
        dma((STEPS, CHUNKS)), dma((STEPS, CHUNKS)), dma((STEPS, CHUNKS)), dma((STEPS, CHUNKS)),
        dma((STEPS, CHUNKS + 2)), dma((STEPS, CHUNKS)), dma((STEPS, CHUNKS)), dma((STEPS, 2)),
        dma((OUTER, CHUNKS)), dma((OUTER, CHUNKS)), dma((OUTER, CHUNKS)), dma((OUTER, CHUNKS)),
        dma((OUTER, CHUNKS)), dma((OUTER, CHUNKS)), dma((OUTER, CHUNKS)), dma((OUTER, CHUNKS)),
    ]
    return pl.pallas_call(
        functools.partial(kernel, (n_series, n_tm), (series, minutes)),
        out_shape=(
            jax.ShapeDtypeStruct(loadings.shape, F32),
            jax.ShapeDtypeStruct(factors.shape, F32),
        ),
        in_specs=[anywhere, anywhere, anywhere, anywhere, pl.BlockSpec(memory_space=vmem)],
        out_specs=(anywhere, anywhere),
        scratch_shapes=scratch,
        compiler_params=pltpu.CompilerParams(
            collective_id=0, has_side_effects=True, vmem_limit_bytes=60 * 1024 * 1024
        ),
        name="factorize",
    )(observed, mask, loadings, factors, lag_weights)


def solution(mesh):
    in_specs = (P("series", "tm"), P("series", "tm"), P("series", None), P("tm", None), P())
    out_specs = (P("series", None), P("tm", None))
    return jax.shard_map(body, mesh=mesh, in_specs=in_specs, out_specs=out_specs, check_vma=False)
```

time: 411 us -> 142 us (0.35)
  Pallas kernels: 0 us -> 137 us
  waiting for transfers between devices: 111 us -> 0 us
  blocking collectives: 105 us -> 0 us
  starting transfers between devices: 101 us -> 0 us
  matrix products: 47.9 us -> 0 us
  local copies, waits for them, and re-layouts: 37.2 us -> 4.13 us
  other arithmetic: 4.57 us -> 0 us
    pallas_call x0 -> x1, Pallas kernels: none -> 137 us  [body(): pl.pallas_call(functools.partial(kernel, (n_series, n_tm), (series, minut...]
    all_to_all x5 -> x0, blocking collectives: 105 us -> none  [the longest x4 70.7 us: copy_for_each(): lax.all_to_all(jnp.broadcast_to(x[None], (devices, *x.shape)), axis, 0, 0...]
    all_to_all x7 -> x0, waiting for transfers between devices: 79.6 us -> none  [the longest x2 47.2 us: copy_for_each(): lax.all_to_all(jnp.broadcast_to(x[None], (devices, *x.shape)), axis, 0, 0...]
    ppermute x24 -> x0, starting transfers between devices: 63.7 us -> none  [shifted(): lax.ppermute(value, axis, [(source, source + steps) for source in range(i...]
    dot_general x10 -> x0, matrix products: 47.9 us -> none  [the longest x4 22.5 us: tile_residual(): lax.dot_general(fb, xb, (((1,), (1,)), ((), ())), preferred_element_type=...]
    all_to_all x7 -> x0, starting transfers between devices: 37 us -> none  [the longest x5 28.2 us: sent_and_summed(): lax.all_to_all(pieces, axis, split_axis=0, concat_axis=0, tiled=True)]
    ppermute x24 -> x0, waiting for transfers between devices: 31.3 us -> none  [shifted(): lax.ppermute(value, axis, [(source, source + steps) for source in range(i...]
    convert_element_type x2 -> x0, local copies, waits for them, and re-layouts: 12.7 us -> none  [tile_residual(): (mask.astype(jnp.float32) * (prod - observed.astype(jnp.float32))).astype...]
  transfers between devices with their start and end apart: 31 -> 0, of which waited for: 11 -> 0; matrix products, arithmetic and copies ran while one was open for 11% -> 0% of each run, Pallas kernels for 0% -> 0%
where the time goes in v1:
time: 142 us
  Pallas kernels  137 us (96%)
  local copies, waits for them, and re-layouts  4.13 us (3%)
    pallas_call x1, Pallas kernels, body(): pl.pallas_call(functools.partial(kernel, (n_series, n_tm), (series, minut...  137 us
    unnamed x2, local copies, waits for them, and re-layouts  4.13 us

profile of v1, /device:TPU:1, one launch (start us, length us, event | category | flops | bytes accessed | tf_op | source)
XLA Modules:
  0.0 141.9 jit_solution(2870966341644744866)
XLA Ops:
  0.6 137.2 %factorize.1 = (f32[2048,128]{1,0:T(8,128)}, f32[1024,128]{1,0:T(8,128)}) custom-call(bf16[2048,1024]{1,0:T(8,128)(2,1)} %obs_hbm.1, bf16[2048,1024]{1,0:T(8,128)(2,1)} %mask_hbm.1, f32[2048,128]{1,0:T(8,128)} %loads_hbm.1, f32[1024,128]{1,0:T(8,128)} %times_hbm.1, f32[2,128]{1,0:T(2,128)} %weights.1), custom_call_target="tpu_custom_call" | custom-call | tf_op jit(solution)/shard_map/factorize/pallas_call | solution.py:369
  137.8 2.3 %copy.9 = f32[2048,128]{1,0:T(8,128)} copy(f32[2048,128]{1,0:T(8,128)} %get-tuple-element.4) | data formatting | bytes 2097152
  140.1 1.9 %copy.10 = f32[1024,128]{1,0:T(8,128)} copy(f32[1024,128]{1,0:T(8,128)} %get-tuple-element.5) | data formatting | bytes 1048576

commit v2 on v1

--- a/solution.py
+++ b/solution.py
@@ -12,6 +12,7 @@
 TIME_STEPS = 2
 STEPS = OUTER * TIME_STEPS
 CHUNKS = 4
+LOAD_CHUNKS = 8
 
 smooth = 4.0
 shrink = 0.1
@@ -29,28 +30,37 @@
 
 def kernel(
     groups, spans,
-    obs_hbm, mask_hbm, loads_hbm, times_hbm, weights,
+    obs_hbm, mask_hbm, loads_hbm, times_hbm, weights_hbm,
     loads_out, times_out,
-    obs, mask, fs, xs, gs, hs, got_g, got_h, core_h, sum_h,
+    obs, mask, weights, fs, xs, gs, hs, got_g, core_h, core_sum, near_h, near_sum, got_h,
     back, ahead, edge_before, edge_after,
     fb, fbt, xb, resid, resid_f, window,
-    in_sem, tile_sem, out_sem,
+    in_sem, tile_sem,
     g_send, g_recv, x_send, x_recv,
     halo_send, back_recv, ahead_recv, edge_recv,
-    core_send, core_recv, h_send, h_recv, f_send, f_recv, pair_send, pair_recv,
+    core_send, core_recv, near_send, near_recv, h_send, h_recv, f_send, f_recv,
+    near_f_send, near_f_recv, core_f_send, core_f_recv,
 ):
     n_series, n_tm = groups
     series, minutes = spans
     rank = weights.shape[1]
-    n_pair = n_tm // 2
+    n_ring = n_tm // 4
+    n_x = 2
+    n_y = n_series // n_x
+    series_offsets = sorted(
+        [(dy, dx) for dx in range(n_x) for dy in range(n_y) if dy or dx],
+        key=lambda at: -min(at[0], n_y - at[0]) - 2 * at[1],
+    )
+    ring_offsets = sorted(range(1, n_ring), key=lambda d: -min(d, n_ring - d))
     cols = minutes // CHUNKS
     own = cols // n_series
     granules = minutes // own
     far = LAG // own
     far_in = far % granules
-    series_rows = series // CHUNKS
+    series_rows = series // LOAD_CHUNKS
     half = series_rows // 2
-    own_f = half // n_pair
+    quarter = half // 2
+    own_f = quarter // n_ring
     total_minutes = minutes * n_tm
     step_time = 1.0 / (series * n_series / rank + margin)
     step_load = 1.0 / total_minutes
@@ -58,8 +68,16 @@
     s = lax.axis_index("series")
     m = lax.axis_index("tm")
     core = lax.rem(m, 2)
-    pair = m // 2
-    partner = m + 1 - 2 * core
+    near = lax.rem(m // 2, 2)
+    ring = m // 4
+    core_peer = m + 1 - 2 * core
+    near_peer = m + 2 - 4 * near
+
+    def series_peer(dy, dx):
+        return n_y * lax.rem(s // n_y + dx, n_x) + lax.rem(s + dy, n_y)
+
+    def ring_peer(d):
+        return 4 * lax.rem(ring + d, n_ring) + 2 * near + core
 
     def send(src, dst, send_sem, recv_sem, to_s, to_m):
         pltpu.make_async_remote_copy(
@@ -75,19 +93,23 @@
     def greet(to_s, to_m):
         pl.semaphore_signal(barrier, inc=1, device_id=(to_s, to_m), device_id_type=MESH)
 
-    for d in range(1, n_series):
-        greet(lax.rem(s + d, n_series), m)
-    for d in range(1, n_pair):
-        greet(s, 2 * lax.rem(pair + d, n_pair) + core)
-    greet(s, partner)
-    greet(s, lax.rem(m + 1, n_tm))
-    greet(s, lax.rem(m + n_tm - 1, n_tm))
-    greetings = (n_series - 1) + (n_pair - 1) + 3
+    for offset in series_offsets:
+        greet(series_peer(*offset), m)
+    for d in ring_offsets:
+        greet(s, ring_peer(d))
+    greet(s, core_peer)
+    greet(s, near_peer)
+    for d in (1, 2):
+        greet(s, lax.rem(m + d, n_tm))
+        greet(s, lax.rem(m + n_tm - d, n_tm))
+    greetings = (n_series - 1) + (n_ring - 1) + 6
 
     times_in = pltpu.make_async_copy(times_hbm, xs.at[0], in_sem.at[0])
     loads_in = pltpu.make_async_copy(loads_hbm, fs.at[0], in_sem.at[1])
+    weights_in = pltpu.make_async_copy(weights_hbm, weights, in_sem.at[2])
     times_in.start()
     loads_in.start()
+    weights_in.start()
 
     def tile_in(c, which):
         ref, hbm = ((obs, obs_hbm), (mask, mask_hbm))[which]
@@ -151,9 +173,11 @@
             resid[part] = (prod - obs[part, at].astype(F32)).astype(BF16) * mask[part, at]
         grad = jnp.dot(fbt[...], resid[...], preferred_element_type=F32)
         gs[k, at] = grad.T
-        for d in range(1, n_series):
-            to = lax.rem(s + d, n_series)
-            send(gs.at[k, rows_of((c * n_series + to) * own, own)], got_g.at[k, c, n_series - 1 - d],
+
+    def share_gradient(k, c):
+        for slot, offset in enumerate(series_offsets):
+            to = series_peer(*offset)
+            send(gs.at[k, rows_of((c * n_series + to) * own, own)], got_g.at[k, c, slot],
                  g_send.at[k, c], g_recv.at[k, c], to, m)
 
     def smoothing(k, c):
@@ -189,20 +213,20 @@
         for d in range(n_series - 1):
             total = total + got_g[k, c, d]
         xs[k + 1, at] = x - step_time * (total + smooth_grad)
-        for d in range(1, n_series):
+        for offset in series_offsets:
             send(xs.at[k + 1, at], xs.at[k + 1, at], x_send.at[k, c], x_recv.at[k, c],
-                 lax.rem(s + d, n_series), m)
+                 series_peer(*offset), m)
         wait_for(got_g.at[k, c], g_send.at[k, c])
 
     def times_arrived(k, c):
         wait_for(got_g.at[k, c], x_recv.at[k, c])
         wait_for(got_g.at[k, c], x_send.at[k, c])
 
-    def each(body):
+    def each(body, count=CHUNKS):
         def step(i, carry):
             body(i)
             return carry
-        lax.fori_loop(0, CHUNKS, step, 0)
+        lax.fori_loop(0, count, step, 0)
 
     def load_gradient(o, e):
         at = rows_of(e * series_rows, series_rows)
@@ -214,48 +238,65 @@
             resid_f[:, part] = (prod - obs[at, part].astype(F32)).astype(BF16) * mask[at, part]
         hs[o, at] = jnp.dot(resid_f[...], xb[...], preferred_element_type=F32)
         send(hs.at[o, rows_of(e * series_rows + half * (1 - core), half)], core_h.at[o, e],
-             core_send.at[o, e], core_recv.at[o, e], s, partner)
-
-    def load_share(o, e):
+             core_send.at[o, e], core_recv.at[o, e], s, core_peer)
+
+    def core_share(o, e):
         wait_for(core_h.at[o, e], core_recv.at[o, e])
-        sum_h[o, e] = hs[o, rows_of(e * series_rows + half * core, half)] + core_h[o, e]
-        for d in range(1, n_pair):
-            to = lax.rem(pair + d, n_pair)
-            send(sum_h.at[o, e, rows_of(to * own_f, own_f)], got_h.at[o, e, n_pair - 1 - d],
-                 h_send.at[o, e], h_recv.at[o, e], s, 2 * to + core)
+        core_sum[o, e] = hs[o, rows_of(e * series_rows + half * core, half)] + core_h[o, e]
+        send(core_sum.at[o, e, rows_of(quarter * (1 - near), quarter)], near_h.at[o, e],
+             near_send.at[o, e], near_recv.at[o, e], s, near_peer)
+
+    def near_share(o, e):
+        wait_for(near_h.at[o, e], near_recv.at[o, e])
+        near_sum[o, e] = core_sum[o, e, rows_of(quarter * near, quarter)] + near_h[o, e]
+        for slot, d in enumerate(ring_offsets):
+            to = lax.rem(ring + d, n_ring)
+            send(near_sum.at[o, e, rows_of(to * own_f, own_f)], got_h.at[o, e, slot],
+                 h_send.at[o, e], h_recv.at[o, e], s, ring_peer(d))
+
+    def quarter_at(e):
+        return e * series_rows + half * core + quarter * near
 
     def update_loads(o, e):
         wait_for(got_h.at[o, e], h_recv.at[o, e])
-        total = sum_h[o, e, rows_of(pair * own_f, own_f)]
-        for d in range(n_pair - 1):
+        total = near_sum[o, e, rows_of(ring * own_f, own_f)]
+        for d in range(n_ring - 1):
             total = total + got_h[o, e, d]
-        at = rows_of(e * series_rows + half * core + pair * own_f, own_f)
+        at = rows_of(quarter_at(e) + ring * own_f, own_f)
         f = fs[o, at]
         fs[o + 1, at] = f - step_load * (total + shrink * f)
-        for d in range(1, n_pair):
-            send(fs.at[o + 1, at], fs.at[o + 1, at], f_send.at[o, e], f_recv.at[o, e],
-                 s, 2 * lax.rem(pair + d, n_pair) + core)
+        for d in ring_offsets:
+            send(fs.at[o + 1, at], fs.at[o + 1, at], f_send.at[o, e], f_recv.at[o, e], s, ring_peer(d))
         wait_for(core_h.at[o, e], core_send.at[o, e])
+        wait_for(near_h.at[o, e], near_send.at[o, e])
         wait_for(got_h.at[o, e], h_send.at[o, e])
 
-    def loads_half(o, e):
+    def quarter_out(o, e):
         wait_for(got_h.at[o, e], f_recv.at[o, e])
+        at = rows_of(quarter_at(e), quarter)
+        send(fs.at[o + 1, at], fs.at[o + 1, at], near_f_send.at[o, e], near_f_recv.at[o, e], s, near_peer)
+        wait_for(got_h.at[o, e], f_send.at[o, e])
+
+    def half_out(o, e):
+        wait_for(near_h.at[o, e], near_f_recv.at[o, e])
         at = rows_of(e * series_rows + half * core, half)
-        send(fs.at[o + 1, at], fs.at[o + 1, at], pair_send.at[o, e], pair_recv.at[o, e], s, partner)
-        wait_for(got_h.at[o, e], f_send.at[o, e])
+        send(fs.at[o + 1, at], fs.at[o + 1, at], core_f_send.at[o, e], core_f_recv.at[o, e], s, core_peer)
+        wait_for(near_h.at[o, e], near_f_send.at[o, e])
 
     def loads_arrived(o, e):
-        wait_for(core_h.at[o, e], pair_recv.at[o, e])
-        wait_for(core_h.at[o, e], pair_send.at[o, e])
+        wait_for(core_h.at[o, e], core_f_recv.at[o, e])
+        wait_for(core_h.at[o, e], core_f_send.at[o, e])
 
     times_in.wait()
     loads_in.wait()
+    weights_in.wait()
     for c in range(CHUNKS):
         round_times(0, c)
+    each(functools.partial(round_loads, 0), LOAD_CHUNKS)
+    for which in range(2):
+        tile_in(0, which).wait()
+    gradient(0, 0)
     pl.semaphore_wait(barrier, greetings)
-    each(lambda c: halo_out(0, c))
-    edges_out(0)
-    each(lambda e: round_loads(0, e))
 
     def outer(o, carry):
         for i in range(TIME_STEPS):
@@ -263,19 +304,33 @@
 
             def first_half(c, k=k, i=i):
                 if i == 0:
-                    @pl.when(o == 0)
+                    @pl.when(jnp.logical_and(o == 0, c > 0))
                     def _():
                         for which in range(2):
                             tile_in(c, which).wait()
+
+                    @pl.when(o + c > 0)
+                    def _():
+                        gradient(k, c)
                 else:
                     times_arrived(k - 1, c)
                     halo_out(k, c)
                     round_times(k, c)
-                gradient(k, c)
+                    gradient(k, c)
+                share_gradient(k, c)
+                if i == 0:
+                    @pl.when(o == 0)
+                    def _():
+                        halo_out(0, lax.rem(c + CHUNKS // 2, CHUNKS))
 
             each(first_half)
             if i > 0:
                 edges_out(k)
+            else:
+                @pl.when(o == 0)
+                def _():
+                    edges_out(0)
+
             for which, ref in enumerate((edge_before, edge_after)):
                 wait_for(ref.at[k], edge_recv.at[k, which])
             each(functools.partial(update_times, k))
@@ -295,17 +350,33 @@
         def _():
             edges_out(k + 1)
 
+        lag = 4
+
         def load_first(e):
             load_gradient(o, e)
 
-            @pl.when(e > 0)
+            @pl.when(e >= lag)
             def _():
-                load_share(o, e - 1)
-
-        each(load_first)
-        load_share(o, CHUNKS - 1)
-        each(functools.partial(update_loads, o))
-        each(functools.partial(loads_half, o))
+                core_share(o, e - lag)
+
+        each(load_first, LOAD_CHUNKS)
+        each(lambda e: core_share(o, e + LOAD_CHUNKS - lag), lag)
+
+        @pl.when(o == OUTER - 1)
+        def _():
+            times_out[...] = xs[STEPS]
+
+        each(functools.partial(near_share, o), LOAD_CHUNKS)
+        each(functools.partial(update_loads, o), LOAD_CHUNKS)
+        def load_back(e):
+            quarter_out(o, e)
+
+            @pl.when(e >= lag)
+            def _():
+                half_out(o, e - lag)
+
+        each(load_back, LOAD_CHUNKS)
+        each(lambda e: half_out(o, e + LOAD_CHUNKS - lag), lag)
 
         def load_last(e):
             loads_arrived(o, e)
@@ -314,16 +385,15 @@
             def _():
                 round_loads(o + 1, e)
 
-        each(load_last)
+            @pl.when(o == OUTER - 1)
+            def _():
+                at = rows_of(e * series_rows, series_rows)
+                loads_out[at] = fs[OUTER, at]
+
+        each(load_last, LOAD_CHUNKS)
         return carry
 
     lax.fori_loop(0, OUTER, outer, 0)
-    times_back = pltpu.make_async_copy(xs.at[STEPS], times_out, out_sem.at[0])
-    loads_back = pltpu.make_async_copy(fs.at[OUTER], loads_out, out_sem.at[1])
-    times_back.start()
-    loads_back.start()
-    times_back.wait()
-    loads_back.wait()
 
 
 def body(observed, mask, loadings, factors, lag_weights):
@@ -332,24 +402,29 @@
     rank = loadings.shape[1]
     cols = minutes // CHUNKS
     own = cols // n_series
-    n_pair = n_tm // 2
-    series_rows = series // CHUNKS
-    half = series_rows // 2
-    own_f = half // n_pair
+    n_ring = n_tm // 4
+    half = series // LOAD_CHUNKS // 2
+    quarter = half // 2
+    own_f = quarter // n_ring
+    arguments = (observed, mask, loadings, factors, lag_weights)
     vmem = pltpu.VMEM
     dma = pltpu.SemaphoreType.DMA
-    anywhere = pl.BlockSpec(memory_space=pl.ANY)
+    hbm = pl.BlockSpec(memory_space=pltpu.HBM)
+    whole = pl.BlockSpec(memory_space=vmem)
     scratch = [
         vmem((series, minutes), BF16),
         vmem((series, minutes), BF16),
+        vmem(lag_weights.shape, F32),
         vmem((OUTER + 1, series, rank), F32),
         vmem((STEPS + 1, minutes, rank), F32),
         vmem((STEPS, minutes, rank), F32),
         vmem((OUTER, series, rank), F32),
         vmem((STEPS, CHUNKS, n_series - 1, own, rank), F32),
-        vmem((OUTER, CHUNKS, n_pair - 1, own_f, rank), F32),
-        vmem((OUTER, CHUNKS, half, rank), F32),
-        vmem((OUTER, CHUNKS, half, rank), F32),
+        vmem((OUTER, LOAD_CHUNKS, half, rank), F32),
+        vmem((OUTER, LOAD_CHUNKS, half, rank), F32),
+        vmem((OUTER, LOAD_CHUNKS, quarter, rank), F32),
+        vmem((OUTER, LOAD_CHUNKS, quarter, rank), F32),
+        vmem((OUTER, LOAD_CHUNKS, n_ring - 1, own_f, rank), F32),
         vmem((STEPS, CHUNKS, own + 8, rank), F32),
         vmem((STEPS, CHUNKS, own + 8, rank), F32),
         vmem((STEPS, 8, rank), F32),
@@ -358,28 +433,26 @@
         vmem((rank, series), BF16),
         vmem((minutes, rank), BF16),
         vmem((series, cols), BF16),
-        vmem((series_rows, minutes), BF16),
+        vmem((series // LOAD_CHUNKS, minutes), BF16),
         vmem((own + 16, rank), F32),
-        dma((2,)), dma((2, CHUNKS)), dma((2,)),
+        dma((3,)), dma((2, CHUNKS)),
         dma((STEPS, CHUNKS)), dma((STEPS, CHUNKS)), dma((STEPS, CHUNKS)), dma((STEPS, CHUNKS)),
         dma((STEPS, CHUNKS + 2)), dma((STEPS, CHUNKS)), dma((STEPS, CHUNKS)), dma((STEPS, 2)),
-        dma((OUTER, CHUNKS)), dma((OUTER, CHUNKS)), dma((OUTER, CHUNKS)), dma((OUTER, CHUNKS)),
-        dma((OUTER, CHUNKS)), dma((OUTER, CHUNKS)), dma((OUTER, CHUNKS)), dma((OUTER, CHUNKS)),
-    ]
+    ] + [dma((OUTER, LOAD_CHUNKS))] * 12
     return pl.pallas_call(
         functools.partial(kernel, (n_series, n_tm), (series, minutes)),
         out_shape=(
             jax.ShapeDtypeStruct(loadings.shape, F32),
             jax.ShapeDtypeStruct(factors.shape, F32),
         ),
-        in_specs=[anywhere, anywhere, anywhere, anywhere, pl.BlockSpec(memory_space=vmem)],
-        out_specs=(anywhere, anywhere),
+        in_specs=[hbm] * len(arguments),
+        out_specs=(whole, whole),
         scratch_shapes=scratch,
         compiler_params=pltpu.CompilerParams(
-            collective_id=0, has_side_effects=True, vmem_limit_bytes=60 * 1024 * 1024
+            collective_id=0, has_side_effects=True, vmem_limit_bytes=50 * 1024 * 1024
         ),
         name="factorize",
-    )(observed, mask, loadings, factors, lag_weights)
+    )(*(pltpu.with_memory_space_constraint(x, pltpu.HBM) for x in arguments))
 
 
 def solution(mesh):

time: 142 us -> 130 us (0.915)
  Pallas kernels: 137 us -> 128 us
  local copies, waits for them, and re-layouts: 4.13 us -> 1.77 us
    pallas_call x1, Pallas kernels: 137 us -> 128 us  [body(): pl.pallas_call(functools.partial(kernel, (n_series, n_tm), (series, minut...]
    unnamed x2, local copies, waits for them, and re-layouts: 4.13 us -> 1.77 us
where the time goes in v2:
time: 130 us
  Pallas kernels  128 us (98%)
  local copies, waits for them, and re-layouts  1.77 us (1%)
    pallas_call x1, Pallas kernels, body(): pl.pallas_call(functools.partial(kernel, (n_series, n_tm), (series, minut...  128 us

profile of v2, /device:TPU:1, one launch (start us, length us, event | category | flops | bytes accessed | tf_op | source)
XLA Modules:
  0.0 130.3 jit_solution(2489629253118861737)
XLA Ops:
  0.6 127.9 %factorize.1 = (f32[2048,128]{1,0:T(8,128)S(1)}, f32[1024,128]{1,0:T(8,128)S(1)}) custom-call(bf16[2048,1024]{1,0:T(8,128)(2,1)} %obs_hbm.1, bf16[2048,1024]{1,0:T(8,128)(2,1)} %mask_hbm.1, f32[2048,128]{1,0:T(8,128)} %loads_hbm.1, f32[1024,128]{1,0:T(8,128)} %times_hbm.1, f32[2,128]{1,0:T(2,128)} %weights_hbm.1), custom_call_target="tpu_custom_call" | custom-call | tf_op jit(solution)/shard_map/factorize/pallas_call | solution.py:442
  128.6 1.0 copy.9
  129.6 0.8 copy.10

commit v3 on v2

--- a/solution.py
+++ b/solution.py
@@ -13,6 +13,7 @@
 STEPS = OUTER * TIME_STEPS
 CHUNKS = 4
 LOAD_CHUNKS = 8
+LOAD_GROUP = 4
 
 smooth = 4.0
 shrink = 0.1
@@ -34,7 +35,7 @@
     loads_out, times_out,
     obs, mask, weights, fs, xs, gs, hs, got_g, core_h, core_sum, near_h, near_sum, got_h,
     back, ahead, edge_before, edge_after,
-    fb, fbt, xb, resid, resid_f, window,
+    fb, fbt, xb, resid, window,
     in_sem, tile_sem,
     g_send, g_recv, x_send, x_recv,
     halo_send, back_recv, ahead_recv, edge_recv,
@@ -228,17 +229,28 @@
             return carry
         lax.fori_loop(0, count, step, 0)
 
-    def load_gradient(o, e):
-        at = rows_of(e * series_rows, series_rows)
-        f_block = fb[at]
+    def load_partial(o, c):
+        at = rows_of(c * cols, cols)
+        x_block = xb[at]
         step = 256
-        for i in range(minutes // step):
+        for i in range(series // step):
             part = pl.ds(i * step, step)
-            prod = lax.dot_general(f_block, xb[part], NT, preferred_element_type=F32)
-            resid_f[:, part] = (prod - obs[at, part].astype(F32)).astype(BF16) * mask[at, part]
-        hs[o, at] = jnp.dot(resid_f[...], xb[...], preferred_element_type=F32)
-        send(hs.at[o, rows_of(e * series_rows + half * (1 - core), half)], core_h.at[o, e],
-             core_send.at[o, e], core_recv.at[o, e], s, core_peer)
+            prod = lax.dot_general(fb[part], x_block, NT, preferred_element_type=F32)
+            resid[part] = (prod - obs[part, at].astype(F32)).astype(BF16) * mask[part, at]
+        hs[o] += jnp.dot(resid[...], x_block, preferred_element_type=F32)
+
+    def load_gradient(o, pair):
+        size = LOAD_GROUP * series_rows
+        at = rows_of(pair * size, size)
+        last = pl.ds(minutes - cols, cols)
+        x_block = xb[last]
+        prod = lax.dot_general(fb[at], x_block, NT, preferred_element_type=F32)
+        rest = (prod - obs[at, last].astype(F32)).astype(BF16) * mask[at, last]
+        hs[o, at] += jnp.dot(rest, x_block, preferred_element_type=F32)
+        for i in range(LOAD_GROUP):
+            e = pair * LOAD_GROUP + i
+            send(hs.at[o, rows_of(e * series_rows + half * (1 - core), half)], core_h.at[o, e],
+                 core_send.at[o, e], core_recv.at[o, e], s, core_peer)
 
     def core_share(o, e):
         wait_for(core_h.at[o, e], core_recv.at[o, e])
@@ -324,6 +336,8 @@
                         halo_out(0, lax.rem(c + CHUNKS // 2, CHUNKS))
 
             each(first_half)
+            if i == 0:
+                hs[o] = jnp.zeros_like(hs[o])
             if i > 0:
                 edges_out(k)
             else:
@@ -344,6 +358,10 @@
             def _():
                 halo_out(k + 1, c)
 
+            @pl.when(c < CHUNKS - 1)
+            def _():
+                load_partial(o, c)
+
         each(settle)
 
         @pl.when(o < OUTER - 1)
@@ -351,16 +369,8 @@
             edges_out(k + 1)
 
         lag = 4
-
-        def load_first(e):
-            load_gradient(o, e)
-
-            @pl.when(e >= lag)
-            def _():
-                core_share(o, e - lag)
-
-        each(load_first, LOAD_CHUNKS)
-        each(lambda e: core_share(o, e + LOAD_CHUNKS - lag), lag)
+        each(functools.partial(load_gradient, o), LOAD_CHUNKS // LOAD_GROUP)
+        each(functools.partial(core_share, o), LOAD_CHUNKS)
 
         @pl.when(o == OUTER - 1)
         def _():
@@ -394,6 +404,17 @@
         return carry
 
     lax.fori_loop(0, OUTER, outer, 0)
+
+
+def copy_out(loads, times, loads_hbm, times_hbm, sem):
+    copies = [
+        pltpu.make_async_copy(loads, loads_hbm, sem.at[0]),
+        pltpu.make_async_copy(times, times_hbm, sem.at[1]),
+    ]
+    for copy in copies:
+        copy.start()
+    for copy in copies:
+        copy.wait()
 
 
 def body(observed, mask, loadings, factors, lag_weights):
@@ -433,13 +454,12 @@
         vmem((rank, series), BF16),
         vmem((minutes, rank), BF16),
         vmem((series, cols), BF16),
-        vmem((series // LOAD_CHUNKS, minutes), BF16),
         vmem((own + 16, rank), F32),
         dma((3,)), dma((2, CHUNKS)),
         dma((STEPS, CHUNKS)), dma((STEPS, CHUNKS)), dma((STEPS, CHUNKS)), dma((STEPS, CHUNKS)),
         dma((STEPS, CHUNKS + 2)), dma((STEPS, CHUNKS)), dma((STEPS, CHUNKS)), dma((STEPS, 2)),
     ] + [dma((OUTER, LOAD_CHUNKS))] * 12
-    return pl.pallas_call(
+    loads, times = pl.pallas_call(
         functools.partial(kernel, (n_series, n_tm), (series, minutes)),
         out_shape=(
             jax.ShapeDtypeStruct(loadings.shape, F32),
@@ -454,6 +474,19 @@
         name="factorize",
     )(*(pltpu.with_memory_space_constraint(x, pltpu.HBM) for x in arguments))
 
+    return pl.pallas_call(
+        copy_out,
+        out_shape=(
+            jax.ShapeDtypeStruct(loadings.shape, F32),
+            jax.ShapeDtypeStruct(factors.shape, F32),
+        ),
+        in_specs=[whole, whole],
+        out_specs=(hbm, hbm),
+        scratch_shapes=[dma((2,))],
+        compiler_params=pltpu.CompilerParams(vmem_limit_bytes=1024 * 1024),
+        name="copy_out",
+    )(loads, times)
+
 
 def solution(mesh):
     in_specs = (P("series", "tm"), P("series", "tm"), P("series", None), P("tm", None), P())

time: 130 us -> 129 us (level)
  local copies, waits for them, and re-layouts: 1.77 us -> 0 us
    unnamed x2 -> x0, local copies, waits for them, and re-layouts: 1.77 us -> none
where the time goes in v3:
time: 129 us
  Pallas kernels  128 us (99%)
    pallas_call x1, Pallas kernels, body(): pl.pallas_call(functools.partial(kernel, (n_series, n_tm), (series, minut...  127 us

profile of v3, /device:TPU:1, one launch (start us, length us, event | category | flops | bytes accessed | tf_op | source)
XLA Modules:
  0.0 128.9 jit_solution(9964814377469131746)
XLA Ops:
  0.6 127.1 %factorize.1 = (f32[2048,128]{1,0:T(8,128)S(1)}, f32[1024,128]{1,0:T(8,128)S(1)}) custom-call(bf16[2048,1024]{1,0:T(8,128)(2,1)} %obs_hbm.1, bf16[2048,1024]{1,0:T(8,128)(2,1)} %mask_hbm.1, f32[2048,128]{1,0:T(8,128)} %loads_hbm.1, f32[1024,128]{1,0:T(8,128)} %times_hbm.1, f32[2,128]{1,0:T(2,128)} %weights_hbm.1), custom_call_target="tpu_custom_call" | custom-call | tf_op jit(solution)/shard_map/factorize/pallas_call | solution.py:462
  127.7 1.2 copy_out.1
